TPU v7x, 64 devices: a 2x2x8 block of a 4x4x8 slice. The times are simulated.
64 devices in a mesh: dp: 4 (over x, y), seq: 16 (over z, core).
Axes of the slice: x: 2, y: 2, z: 8, core: 2. Of those that a mesh axis runs over, the one named last changes fastest.
The devices are a block of a 4x4x8 slice.
Arguments:
- enc_out: bfloat16 [64, 384, 1024], P('dp', 'seq'), parts along dimension 0
- pred_out: bfloat16 [64, 24, 320], P('dp'), parts along dimension 0
- w_enc: bfloat16 [1024, 512], replicated
- w_pred: bfloat16 [320, 512], replicated
- w_out: bfloat16 [512, 1024], replicated
- b_out: float32 [1024], replicated
- labels: int32 [64, 23], P('dp'), parts along dimension 0
- frame_len: int32 [64], P('dp'), parts along dimension 0
- label_len: int32 [64], P('dp'), parts along dimension 0
Outputs:
- output: float32 [64], P('dp'), parts along dimension 0
There are 4 independent parts. A program takes and returns all parts, laid end to end along the dimension named above; an argument that names none is the same for every part.
All inputs are finite; a program needn't handle non-finite values.
Results may differ from a plain program's by a relative error of at most 0.001.
Values are sent between devices in bfloat16 or wider.
A program may use at most 768 MiB of HBM per device.

v0:
```python
import functools
import jax
import jax.numpy as jnp
from jax import lax
from jax.experimental import pallas as pl
from jax.experimental.pallas import tpu as pltpu
from jax.sharding import PartitionSpec as P

NEG_FILL = -1.0e30
OCT = 8
ITEMS = 32
GROUP = 32
MESH = pl.DeviceIdType.MESH


def joint_kernel(enc_hbm, pred_hbm, wenc_hbm, wpred_hbm, wout_hbm, bout_hbm, lab_hbm, flen_hbm, llen_hbm,
                 m_out,
                 enc_v, pred_v, wenc_v, wpred_v, wout_v, bout_v, lab_raw, lab_v, flen_s, llen_s,
                 w_t, bias_t, a_v, c_v, hid, z_v, blank_d, label_d, turn_v, tab_v, tab_s, sems, tab_sem):
    n_utt, n_lab = lab_hbm.shape
    n_pos = n_lab + 1
    t_local = enc_v.shape[0] // n_utt
    n_oct = t_local // OCT
    joint, vocab = wout_v.shape
    n_slab = joint // 128
    rep = 128 // n_utt
    t0 = lax.axis_index("seq") * t_local

    copies = [
        pltpu.make_async_copy(src, dst, sems.at[k])
        for k, (src, dst) in enumerate([
            (flen_hbm, flen_s), (llen_hbm, llen_s), (lab_hbm, lab_raw), (bout_hbm, bout_v),
            (wout_hbm, wout_v), (enc_hbm, enc_v), (wenc_hbm, wenc_v), (pred_hbm, pred_v), (wpred_hbm, wpred_v)])
    ]
    for copy in copies:
        copy.start()

    blank_d[...] = jnp.zeros_like(blank_d)
    label_d[...] = jnp.full(label_d.shape, NEG_FILL, jnp.float32)

    for copy in copies[:3]:
        copy.wait()
    lab_v[...] = jnp.zeros_like(lab_v)
    lab_v[:, :n_lab] = lab_raw[...]
    shape = tab_v.shape[1:]
    cums, nus, total = [], [], jnp.int32(0)
    for b in range(n_utt):
        n_t = jnp.clip((flen_s[b] - t0 + OCT - 1) // OCT, 0, n_oct)
        cums.append(total)
        nus.append(llen_s[b] + 1)
        total = total + n_t * nus[b]
    lane = lax.broadcasted_iota(jnp.int32, shape, 1)
    item = lax.broadcasted_iota(jnp.int32, shape, 0) * ITEMS + lane % ITEMS
    item = jnp.minimum(item, total - 1)
    utt = jnp.zeros(shape, jnp.int32)
    base = jnp.zeros(shape, jnp.int32)
    width = jnp.ones(shape, jnp.int32)
    frames = jnp.zeros(shape, jnp.int32)
    for b in range(n_utt):
        hit = item >= cums[b]
        utt = jnp.where(hit, b, utt)
        base = jnp.where(hit, cums[b], base)
        width = jnp.where(hit, nus[b], width)
        frames = jnp.where(hit, flen_s[b] - t0, frames)
    rest = item - base
    octet = jnp.zeros(shape, jnp.int32)
    for k in range(1, n_oct):
        octet = octet + jnp.where(rest >= k * width, 1, 0)
    pos = jnp.clip(rest - octet * width, 0, n_pos - 1)
    word = jnp.zeros(shape, jnp.int32)
    for b in range(n_utt):
        row = jnp.broadcast_to(lab_v[b:b + 1, :], shape)
        word = jnp.where(utt == b, jnp.take_along_axis(row, pos, axis=1, mode="promise_in_bounds"), word)
    has_label = pos < width - 1
    word = jnp.where(has_label, word, 0)
    field = lane // ITEMS
    tab_v[0] = jnp.where(field == 0, utt * t_local + octet * OCT,
                         jnp.where(field == 1, utt * n_pos + pos,
                                   jnp.where(field == 2, word, (octet * n_pos + pos) * OCT)))
    tab_v[1] = jnp.where(field == 0, utt, jnp.where(field == 1, jnp.where(has_label, utt, -1), frames - octet * OCT))
    tab_copy = pltpu.make_async_copy(tab_v, tab_s, tab_sem)
    tab_copy.start()

    copies[3].wait()
    copies[4].wait()
    top_bias = jnp.max(bout_v[...])
    spread = jnp.zeros((8, 128), jnp.float32)
    for k in range(vocab // 128):
        cols = pl.ds(k * 128, 128)
        w_t[cols, :] = wout_v[:, cols].T
        bias_t[cols, :] = jnp.broadcast_to(bout_v[k:k + 1, :] - top_bias, (128, 128)).T
        mass = jnp.sum(jnp.abs(wout_v[:, cols].astype(jnp.float32)).reshape(joint // 8, 8, 128), axis=0)
        spread = jnp.maximum(spread, jnp.sum(mass, axis=0, keepdims=True))
    narrow = jnp.max(spread) <= 60.0
    copies[5].wait()
    copies[6].wait()
    proj = jnp.dot(enc_v[...], wenc_v[...], preferred_element_type=jnp.float32).astype(jnp.bfloat16).astype(jnp.float32)
    for s in range(n_slab):
        a_v[s] = proj[:, 128 * s:128 * s + 128]
    copies[7].wait()
    copies[8].wait()
    proj = jnp.dot(pred_v[...], wpred_v[...], preferred_element_type=jnp.float32).astype(jnp.bfloat16).astype(jnp.float32)
    for s in range(n_slab):
        c_v[s] = proj[:, 128 * s:128 * s + 128]
    tab_copy.wait()

    lane8 = lax.broadcasted_iota(jnp.int32, (OCT, 128), 1)
    frame8 = lax.broadcasted_iota(jnp.int32, (OCT, 128), 0)
    lane_utt = lane8 // rep
    lane_item = lax.broadcasted_iota(jnp.int32, (1, 128), 1) // OCT

    def make_hidden(tile):
        for q in range(ITEMS // 2):
            for s in range(n_slab):
                parts = []
                for k in (2 * q, 2 * q + 1):
                    a_row = pl.multiple_of(tab_s[0, tile, k], OCT)
                    parts.append(a_v[s, pl.ds(a_row, OCT), :] + c_v[s, pl.ds(tab_s[0, tile, ITEMS + k], 1), :])
                hid[16 * q:16 * q + 16, 128 * s:128 * s + 128] = jnp.tanh(
                    jnp.concatenate(parts, axis=0)).astype(jnp.bfloat16)

    def finish(tile, with_max):
        for g in range(2):
            label_z = jnp.zeros((1, 128), jnp.float32)
            for k in range(16):
                y = tab_s[0, tile, 2 * ITEMS + 16 * g + k]
                label_z = jnp.where(lane_item == k, z_v[g, pl.ds(y, 1), :] + bias_t[pl.ds(y, 1), :], label_z)
            blank_z = z_v[g, 0:1, :] + bias_t[0:1, :]
            top = jnp.zeros((1, 128), jnp.float32)
            if with_max:
                part = jnp.full((8, 128), NEG_FILL, jnp.float32)
                for k in range(vocab // 128):
                    rows = slice(k * 128, k * 128 + 128)
                    part = jnp.maximum(part, jnp.max((z_v[g, rows, :] + bias_t[rows, :]).reshape(16, 8, 128), axis=0))
                top = jnp.max(part, axis=0, keepdims=True)
            part = jnp.zeros((8, 128), jnp.float32)
            for k in range(vocab // 128):
                rows = slice(k * 128, k * 128 + 128)
                logit = z_v[g, rows, :] + bias_t[rows, :]
                if with_max:
                    logit = logit - top
                part = part + jnp.sum(jnp.exp(logit).reshape(16, 8, 128), axis=0)
            lse = jnp.log(jnp.sum(part, axis=0, keepdims=True)) + top
            blank_lp = jnp.broadcast_to(blank_z - lse, (OCT, 128))
            label_lp = jnp.broadcast_to(label_z - lse, (OCT, 128))
            for k in range(16):
                j = 16 * g + k
                live = frame8 < tab_s[1, tile, 2 * ITEMS + j]
                row = pl.ds(pl.multiple_of(tab_s[0, tile, 3 * ITEMS + j], OCT), OCT)
                pick = frame8 + OCT * k
                value = jnp.take_along_axis(blank_lp, pick, axis=1, mode="promise_in_bounds")
                pltpu.store(blank_d.at[row, :], value, mask=(lane_utt == tab_s[1, tile, j]) & live)
                value = jnp.take_along_axis(label_lp, pick, axis=1, mode="promise_in_bounds")
                pltpu.store(label_d.at[row, :], value, mask=(lane_utt == tab_s[1, tile, ITEMS + j]) & live)

    def matmul():
        z = lax.dot_general(w_t[...], hid[...], (((1,), (1,)), ((), ())), preferred_element_type=jnp.float32)
        z_v[0] = z[:, :128]
        z_v[1] = z[:, 128:]

    n_tiles = (total + ITEMS - 1) // ITEMS

    def run_tiles(with_max):
        make_hidden(0)
        matmul()
        make_hidden(jnp.minimum(1, n_tiles - 1))

        def step(i, _):
            finish(i - 1, with_max)
            matmul()
            make_hidden(jnp.minimum(i + 1, n_tiles - 1))
            return 0

        lax.fori_loop(1, n_tiles, step, 0)
        finish(n_tiles - 1, with_max)

    @pl.when((n_tiles > 0) & narrow)
    def _():
        run_tiles(False)

    @pl.when((n_tiles > 0) & jnp.logical_not(narrow))
    def _():
        run_tiles(True)

    entry = frame8 * rep + lane8 % rep
    stay = [jnp.where(entry == u, 0.0, NEG_FILL) for u in range(n_pos)]
    move = [None] * n_pos
    for d in range(t_local + n_pos - 1):
        for u in range(min(d, n_pos - 1), max(d - t_local, -1), -1):
            t = d - u
            row = (t // OCT * n_pos + u) * OCT + t % OCT
            if u == 0:
                alpha = stay[0]
            else:
                high, low = jnp.maximum(stay[u], move[u - 1]), jnp.minimum(stay[u], move[u - 1])
                alpha = high + jnp.log(1.0 + jnp.exp(low - high))
            stay[u] = alpha + blank_d[row:row + 1, :]
            move[u] = alpha + label_d[row:row + 1, :]
    for u in range(n_pos):
        for j in range(n_pos // rep):
            turn_v[GROUP * j + u:GROUP * j + u + 1, :] = stay[u][j:j + 1, :]
    turned = turn_v[...].T
    per = 128 // GROUP
    group = lane8 // GROUP
    for h in range(n_utt // per):
        for j in range(n_pos // rep):
            out = None
            for q in range(per):
                b = per * h + q
                piece = turned[rep * b:rep * b + rep, :]
                if q != j:
                    piece = pltpu.roll(piece, (GROUP * (q - j)) % 128, 1)
                out = piece if out is None else jnp.where(group == q, piece, out)
            m_out[h, rep * j:rep * j + rep, :] = out


def lattice_kernel(n_seq, m_hbm, llen_hbm, loss_ref,
                   m_recv, llen_s, v_out, v_recv, send_sem, recv_sem, out_sem, in_sem, own_sem):
    n_hand, n_pos = m_hbm.shape[:2]
    n_utt = llen_hbm.shape[0]
    per = 128 // GROUP
    me = lax.axis_index("seq")
    mine = me < n_hand
    my_hand = jnp.minimum(me, n_hand - 1)

    barrier = pltpu.get_barrier_semaphore()

    def greet(other):
        pl.semaphore_signal(barrier, inc=1, device_id={"seq": other}, device_id_type=MESH)

    @pl.when(mine)
    def _():
        for d in range(n_seq):
            @pl.when(me != d)
            def _():
                greet(d)

    own_len = pltpu.make_async_copy(llen_hbm, llen_s, own_sem.at[0])
    own_matrix = pltpu.make_async_copy(m_hbm.at[my_hand], m_recv.at[me], own_sem.at[1])

    @pl.when(mine)
    def _():
        own_len.start()
        own_matrix.start()

    pl.semaphore_wait(barrier, jnp.where(mine, n_hand - 1, n_hand))

    def send_matrix(h):
        return pltpu.make_async_remote_copy(
            src_ref=m_hbm.at[h], dst_ref=m_recv.at[me], send_sem=send_sem.at[h], recv_sem=recv_sem.at[me],
            device_id={"seq": h}, device_id_type=MESH)

    for h in range(n_hand):
        @pl.when(me != h)
        def _():
            send_matrix(h).start()

    def send_row(d):
        return pltpu.make_async_remote_copy(
            src_ref=v_out, dst_ref=v_recv.at[my_hand], send_sem=out_sem.at[d], recv_sem=in_sem.at[my_hand],
            device_id={"seq": d}, device_id_type=MESH)

    @pl.when(mine)
    def _():
        own_len.wait()
        own_matrix.wait()

        def arrived(src):
            @pl.when(src != me)
            def _():
                pltpu.make_async_remote_copy(
                    src_ref=m_hbm.at[0], dst_ref=m_recv.at[src], send_sem=send_sem.at[0], recv_sem=recv_sem.at[src],
                    device_id={"seq": src}, device_id_type=MESH).wait_recv()

        sub = lax.broadcasted_iota(jnp.int32, (n_pos, 128), 0)
        lane = lax.broadcasted_iota(jnp.int32, (n_pos, 128), 1)
        turn_idx = lane // GROUP * GROUP + sub

        def join(src, row):
            arrived(src)
            col = jnp.take_along_axis(jnp.broadcast_to(row, (n_pos, 128)), turn_idx, axis=1, mode="promise_in_bounds")
            terms = col + m_recv[src]
            top = jnp.max(terms, axis=0, keepdims=True)
            return top + jnp.log(jnp.sum(jnp.exp(terms - top), axis=0, keepdims=True))

        arrived(jnp.int32(0))
        row = m_recv[0, 0:1, :]
        row = lax.fori_loop(1, n_seq, join, row)
        sub8 = lax.broadcasted_iota(jnp.int32, (8, 128), 0)
        lane8 = lax.broadcasted_iota(jnp.int32, (8, 128), 1)
        want = jnp.full((8, 128), -1, jnp.int32)
        for b in range(n_utt):
            want = jnp.where(my_hand * per + sub8 == b, llen_s[b], want)
        keep = (lane8 // GROUP == sub8) & (lane8 % GROUP == want)
        column = jnp.sum(jnp.where(keep, row, 0.0), axis=1, keepdims=True)
        here = (lane8 == my_hand * per + sub8) & (sub8 < per)
        v_out[...] = jnp.sum(jnp.where(here, column, 0.0), axis=0, keepdims=True)
        for d in range(n_seq):
            @pl.when(me != d)
            def _():
                send_row(d).start()
        v_recv[my_hand] = v_out[...]

    for h in range(n_hand):
        @pl.when(me != h)
        def _():
            pltpu.make_async_remote_copy(
                src_ref=v_out, dst_ref=v_recv.at[h], send_sem=out_sem.at[0], recv_sem=in_sem.at[h],
                device_id={"seq": h}, device_id_type=MESH).wait_recv()
    total = v_recv[0]
    for h in range(1, n_hand):
        total = total + v_recv[h]
    loss_ref[...] = -total[0, :n_utt]

    for h in range(n_hand):
        @pl.when(me != h)
        def _():
            send_matrix(h).wait_send()

    @pl.when(mine)
    def _():
        for d in range(n_seq):
            @pl.when(me != d)
            def _():
                send_row(d).wait_send()


def joint_call(enc_blk, pred_out, w_enc, w_pred, w_out, b_out, labels, frame_len, label_len):
    n_utt, t_local, d_enc = enc_blk.shape
    n_pos, d_pred = pred_out.shape[1:]
    joint, vocab = w_out.shape
    n_oct = t_local // OCT
    n_slab = joint // 128
    per = 128 // GROUP
    tab_rows = -(-(n_utt * n_pos * n_oct // ITEMS + 1) // 8) * 8
    hbm = pl.BlockSpec(memory_space=pl.ANY)
    vmem = pl.BlockSpec(memory_space=pltpu.VMEM)
    f32, bf16, i32 = jnp.float32, jnp.bfloat16, jnp.int32
    return pl.pallas_call(
        joint_kernel,
        out_shape=pltpu.VMEM((n_utt // per, n_pos, 128), f32),
        in_specs=[hbm] * 9,
        out_specs=vmem,
        scratch_shapes=[
            pltpu.VMEM((n_utt * t_local, d_enc), bf16),
            pltpu.VMEM((n_utt * n_pos, d_pred), bf16),
            pltpu.VMEM((d_enc, joint), bf16),
            pltpu.VMEM((d_pred, joint), bf16),
            pltpu.VMEM((joint, vocab), bf16),
            pltpu.VMEM((vocab // 128, 128), f32),
            pltpu.VMEM((n_utt, n_pos - 1), i32),
            pltpu.VMEM((n_utt, 128), i32),
            pltpu.SMEM((n_utt,), i32),
            pltpu.SMEM((n_utt,), i32),
            pltpu.VMEM((vocab, joint), bf16),
            pltpu.VMEM((vocab, 128), f32),
            pltpu.VMEM((n_slab, n_utt * t_local, 128), f32),
            pltpu.VMEM((n_slab, n_utt * n_pos, 128), f32),
            pltpu.VMEM((ITEMS * OCT, joint), bf16),
            pltpu.VMEM((2, vocab, 128), f32),
            pltpu.VMEM((t_local * n_pos, 128), f32),
            pltpu.VMEM((t_local * n_pos, 128), f32),
            pltpu.VMEM((128, 128), f32),
            pltpu.VMEM((2, tab_rows, 128), i32),
            pltpu.SMEM((2, tab_rows, 128), i32),
            pltpu.SemaphoreType.DMA((9,)),
            pltpu.SemaphoreType.DMA,
        ],
        name="joint",
    )(enc_blk.reshape(n_utt * t_local, d_enc), pred_out.reshape(n_utt * n_pos, d_pred), w_enc, w_pred, w_out,
      b_out.reshape(vocab // 128, 128), labels, frame_len, label_len)


def lattice_call(n_seq, matrices, label_len):
    n_hand, n_pos = matrices.shape[:2]
    n_utt = label_len.shape[0]
    f32 = jnp.float32
    return pl.pallas_call(
        functools.partial(lattice_kernel, n_seq),
        out_shape=pltpu.VMEM((n_utt,), f32),
        in_specs=[pl.BlockSpec(memory_space=pltpu.VMEM), pl.BlockSpec(memory_space=pl.ANY)],
        out_specs=pl.BlockSpec(memory_space=pltpu.VMEM),
        scratch_shapes=[
            pltpu.VMEM((n_seq, n_pos, 128), f32),
            pltpu.SMEM((n_utt,), jnp.int32),
            pltpu.VMEM((1, 128), f32),
            pltpu.VMEM((n_hand, 1, 128), f32),
            pltpu.SemaphoreType.DMA((n_hand,)),
            pltpu.SemaphoreType.DMA((n_seq,)),
            pltpu.SemaphoreType.DMA((n_seq,)),
            pltpu.SemaphoreType.DMA((n_hand,)),
            pltpu.SemaphoreType.DMA((2,)),
        ],
        compiler_params=pltpu.CompilerParams(collective_id=0, has_side_effects=True),
        name="lattice",
    )(matrices, label_len)


def solution(mesh):
    n_seq = mesh.shape["seq"]

    def local_loss(enc_blk, pred_out, w_enc, w_pred, w_out, b_out, labels, frame_len, label_len):
        matrices = joint_call(enc_blk, pred_out, w_enc, w_pred, w_out, b_out, labels, frame_len, label_len)
        return lattice_call(n_seq, pltpu.with_memory_space_constraint(matrices, pltpu.VMEM), label_len)

    in_specs = (P("dp", "seq", None), P("dp", None, None), P(), P(), P(), P(), P("dp", None), P("dp"), P("dp"))
    return jax.shard_map(local_loss, mesh=mesh, in_specs=in_specs, out_specs=P("dp"), check_vma=False)
```

profile of v0, /device:TPU:21, one launch (start us, length us, event | category | flops | bytes accessed | tf_op | source)
XLA Modules:
  0.0 36.0 jit_solution(7339525372700127389)
XLA Ops:
  0.0 19.8 %joint.1.m_hbm = f32[4,24,128]{2,1,0:T(8,128)S(1)} custom-call(bf16[384,1024]{1,0:T(8,128)(2,1)} %bitcast.3, bf16[384,320]{1,0:T(8,128)(2,1)} %bitcast.4, bf16[1024,512]{1,0:T(8,128)(2,1)} %wenc_hbm.1, bf16[320,512]{1,0:T(8,128)(2,1)} %wpred_hbm.1, bf16[512,1024]{1,0:T(8,128)(2,1)} %wout_hbm.1, f32[8,128]{1,0:T(8,128)} %bitcast.5, s32[16,23]{1,0:T(8,128)} %lab_hbm.1, ...), custom_call_target="tpu_custom_call" | custom-call | tf_op jit(solution)/shard_map/joint/pallas_call | solution.py:339
  19.8 15.7 %lattice.1 = f32[16]{0:T(128)S(1)} custom-call(f32[4,24,128]{2,1,0:T(8,128)S(1)} %joint.1.m_hbm, s32[16]{0:T(128)} %llen_hbm.3), custom_call_target="tpu_custom_call" | custom-call | tf_op jit(solution)/shard_map/lattice/pallas_call | solution.py:378
  35.4 0.5 %copy.11 = f32[16]{0:T(128)} copy(f32[16]{0:T(128)S(1)} %lattice.1) | data formatting | bytes 128
where the time goes:
time: 36 us
  Pallas kernels  35.4 us (98%)
  local copies, waits for them, and re-layouts  0.51 us (1%)
    pallas_call x1, Pallas kernels, joint_call(): pl.pallas_call(joint_kernel, out_shape=pltpu.VMEM((n_utt // per, n_pos, 1...  19.8 us
    pallas_call x1, Pallas kernels, lattice_call(): pl.pallas_call(functools.partial(lattice_kernel, n_seq), out_shape=pltpu....  15.7 us

commit v1 on v0

--- a/solution.py
+++ b/solution.py
@@ -16,14 +16,15 @@
 def joint_kernel(enc_hbm, pred_hbm, wenc_hbm, wpred_hbm, wout_hbm, bout_hbm, lab_hbm, flen_hbm, llen_hbm,
                  m_out,
                  enc_v, pred_v, wenc_v, wpred_v, wout_v, bout_v, lab_raw, lab_v, flen_s, llen_s,
-                 w_t, bias_t, a_v, c_v, hid, z_v, blank_d, label_d, turn_v, tab_v, tab_s, sems, tab_sem):
+                 w_t, bias_t, a_v, c_v, hid, z_v, lp_v, both_d, blank_d, label_d, turn_v, tab_v, tab_s, sems, tab_sem):
     n_utt, n_lab = lab_hbm.shape
     n_pos = n_lab + 1
     t_local = enc_v.shape[0] // n_utt
     n_oct = t_local // OCT
     joint, vocab = wout_v.shape
     n_slab = joint // 128
-    rep = 128 // n_utt
+    half = 64
+    rep = half // n_utt
     t0 = lax.axis_index("seq") * t_local
 
     copies = [
@@ -35,8 +36,7 @@
     for copy in copies:
         copy.start()
 
-    blank_d[...] = jnp.zeros_like(blank_d)
-    label_d[...] = jnp.full(label_d.shape, NEG_FILL, jnp.float32)
+    both_d[...] = jnp.where(lax.broadcasted_iota(jnp.int32, both_d.shape, 1) < half, 0.0, NEG_FILL)
 
     for copy in copies[:3]:
         copy.wait()
@@ -55,13 +55,11 @@
     utt = jnp.zeros(shape, jnp.int32)
     base = jnp.zeros(shape, jnp.int32)
     width = jnp.ones(shape, jnp.int32)
-    frames = jnp.zeros(shape, jnp.int32)
     for b in range(n_utt):
         hit = item >= cums[b]
         utt = jnp.where(hit, b, utt)
         base = jnp.where(hit, cums[b], base)
         width = jnp.where(hit, nus[b], width)
-        frames = jnp.where(hit, flen_s[b] - t0, frames)
     rest = item - base
     octet = jnp.zeros(shape, jnp.int32)
     for k in range(1, n_oct):
@@ -71,19 +69,20 @@
     for b in range(n_utt):
         row = jnp.broadcast_to(lab_v[b:b + 1, :], shape)
         word = jnp.where(utt == b, jnp.take_along_axis(row, pos, axis=1, mode="promise_in_bounds"), word)
-    has_label = pos < width - 1
-    word = jnp.where(has_label, word, 0)
+    word = jnp.where(pos < width - 1, word, vocab)
     field = lane // ITEMS
     tab_v[0] = jnp.where(field == 0, utt * t_local + octet * OCT,
                          jnp.where(field == 1, utt * n_pos + pos,
                                    jnp.where(field == 2, word, (octet * n_pos + pos) * OCT)))
-    tab_v[1] = jnp.where(field == 0, utt, jnp.where(field == 1, jnp.where(has_label, utt, -1), frames - octet * OCT))
+    tab_v[1] = utt
     tab_copy = pltpu.make_async_copy(tab_v, tab_s, tab_sem)
     tab_copy.start()
 
     copies[3].wait()
     copies[4].wait()
     top_bias = jnp.max(bout_v[...])
+    bias_t[vocab:, :] = jnp.full((8, 128), NEG_FILL, jnp.float32)
+    z_v[:, :, vocab:, :] = jnp.zeros((2, 2, 8, 128), jnp.float32)
     spread = jnp.zeros((8, 128), jnp.float32)
     for k in range(vocab // 128):
         cols = pl.ds(k * 128, 128)
@@ -106,81 +105,114 @@
 
     lane8 = lax.broadcasted_iota(jnp.int32, (OCT, 128), 1)
     frame8 = lax.broadcasted_iota(jnp.int32, (OCT, 128), 0)
-    lane_utt = lane8 // rep
+    lane_utt = lane8 % half // rep
     lane_item = lax.broadcasted_iota(jnp.int32, (1, 128), 1) // OCT
 
-    def make_hidden(tile):
+    def make_hidden(tile, slot):
         for q in range(ITEMS // 2):
+            pair = (2 * q, 2 * q + 1)
+            a_rows = [pl.ds(pl.multiple_of(tab_s[0, tile, k], OCT), OCT) for k in pair]
+            c_rows = [pl.ds(tab_s[0, tile, ITEMS + k], 1) for k in pair]
             for s in range(n_slab):
-                parts = []
-                for k in (2 * q, 2 * q + 1):
-                    a_row = pl.multiple_of(tab_s[0, tile, k], OCT)
-                    parts.append(a_v[s, pl.ds(a_row, OCT), :] + c_v[s, pl.ds(tab_s[0, tile, ITEMS + k], 1), :])
-                hid[16 * q:16 * q + 16, 128 * s:128 * s + 128] = jnp.tanh(
-                    jnp.concatenate(parts, axis=0)).astype(jnp.bfloat16)
-
-    def finish(tile, with_max):
+                total_in = [a_v[s, a_row, :] + c_v[s, c_row, :] for a_row, c_row in zip(a_rows, c_rows)]
+                hid[slot, 16 * q:16 * q + 16, 128 * s:128 * s + 128] = jnp.tanh(
+                    jnp.concatenate(total_in, axis=0)).astype(jnp.bfloat16)
+
+    def finish(tile, slot, with_max):
         for g in range(2):
             label_z = jnp.zeros((1, 128), jnp.float32)
             for k in range(16):
-                y = tab_s[0, tile, 2 * ITEMS + 16 * g + k]
-                label_z = jnp.where(lane_item == k, z_v[g, pl.ds(y, 1), :] + bias_t[pl.ds(y, 1), :], label_z)
-            blank_z = z_v[g, 0:1, :] + bias_t[0:1, :]
+                y = pl.ds(tab_s[0, tile, 2 * ITEMS + 16 * g + k], 1)
+                label_z = jnp.where(lane_item == k, z_v[slot, g, y, :] + bias_t[y, :], label_z)
+            blank_z = z_v[slot, g, 0:1, :] + bias_t[0:1, :]
             top = jnp.zeros((1, 128), jnp.float32)
             if with_max:
                 part = jnp.full((8, 128), NEG_FILL, jnp.float32)
                 for k in range(vocab // 128):
                     rows = slice(k * 128, k * 128 + 128)
-                    part = jnp.maximum(part, jnp.max((z_v[g, rows, :] + bias_t[rows, :]).reshape(16, 8, 128), axis=0))
+                    part = jnp.maximum(
+                        part, jnp.max((z_v[slot, g, rows, :] + bias_t[rows, :]).reshape(16, 8, 128), axis=0))
                 top = jnp.max(part, axis=0, keepdims=True)
             part = jnp.zeros((8, 128), jnp.float32)
             for k in range(vocab // 128):
                 rows = slice(k * 128, k * 128 + 128)
-                logit = z_v[g, rows, :] + bias_t[rows, :]
+                logit = z_v[slot, g, rows, :] + bias_t[rows, :]
                 if with_max:
                     logit = logit - top
                 part = part + jnp.sum(jnp.exp(logit).reshape(16, 8, 128), axis=0)
             lse = jnp.log(jnp.sum(part, axis=0, keepdims=True)) + top
-            blank_lp = jnp.broadcast_to(blank_z - lse, (OCT, 128))
-            label_lp = jnp.broadcast_to(label_z - lse, (OCT, 128))
+            lp_v[slot, g, 0:1, :] = blank_z - lse
+            lp_v[slot, g, 1:2, :] = label_z - lse
+
+    def place(tile, slot):
+        for g in range(2):
+            wide = jnp.concatenate([jnp.broadcast_to(lp_v[slot, g, 0:1, :], (half, 128)),
+                                    jnp.broadcast_to(lp_v[slot, g, 1:2, :], (half, 128))], axis=0).T
             for k in range(16):
-                j = 16 * g + k
-                live = frame8 < tab_s[1, tile, 2 * ITEMS + j]
-                row = pl.ds(pl.multiple_of(tab_s[0, tile, 3 * ITEMS + j], OCT), OCT)
-                pick = frame8 + OCT * k
-                value = jnp.take_along_axis(blank_lp, pick, axis=1, mode="promise_in_bounds")
-                pltpu.store(blank_d.at[row, :], value, mask=(lane_utt == tab_s[1, tile, j]) & live)
-                value = jnp.take_along_axis(label_lp, pick, axis=1, mode="promise_in_bounds")
-                pltpu.store(label_d.at[row, :], value, mask=(lane_utt == tab_s[1, tile, ITEMS + j]) & live)
-
-    def matmul():
-        z = lax.dot_general(w_t[...], hid[...], (((1,), (1,)), ((), ())), preferred_element_type=jnp.float32)
-        z_v[0] = z[:, :128]
-        z_v[1] = z[:, 128:]
+                row = pl.ds(pl.multiple_of(tab_s[0, tile, 3 * ITEMS + 16 * g + k], OCT), OCT)
+                pltpu.store(both_d.at[row, :], wide[OCT * k:OCT * k + OCT, :],
+                            mask=lane_utt == tab_s[1, tile, 16 * g + k])
+
+    def matmul(slot):
+        z = lax.dot_general(w_t[...], hid[slot], (((1,), (1,)), ((), ())), preferred_element_type=jnp.float32)
+        for g in range(2):
+            z_v[slot, g, :vocab, :] = z[:, 128 * g:128 * g + 128]
 
     n_tiles = (total + ITEMS - 1) // ITEMS
 
-    def run_tiles(with_max):
-        make_hidden(0)
-        matmul()
-        make_hidden(jnp.minimum(1, n_tiles - 1))
-
-        def step(i, _):
-            finish(i - 1, with_max)
-            matmul()
-            make_hidden(jnp.minimum(i + 1, n_tiles - 1))
+    @pl.when((n_tiles > 0) & narrow)
+    def _():
+        make_hidden(0, 0)
+        matmul(0)
+        make_hidden(1, 1)
+
+        def two_tiles(p, _):
+            i = 2 * p + 1
+            place(jnp.maximum(i - 2, 1), 1)
+            place(jnp.maximum(i - 3, 0), 0)
+            finish(i - 1, 0, False)
+            matmul(1)
+            make_hidden(i + 1, 0)
+            finish(i, 1, False)
+            matmul(0)
+            make_hidden(i + 2, 1)
             return 0
 
-        lax.fori_loop(1, n_tiles, step, 0)
-        finish(n_tiles - 1, with_max)
-
-    @pl.when((n_tiles > 0) & narrow)
-    def _():
-        run_tiles(False)
+        n_pairs = (n_tiles - 1) // 2
+        lax.fori_loop(0, n_pairs, two_tiles, 0)
+        place(jnp.maximum(2 * n_pairs - 1, 1), 1)
+        place(jnp.maximum(2 * n_pairs - 2, 0), 0)
+        finish(2 * n_pairs, 0, False)
+
+        @pl.when(n_tiles % 2 == 0)
+        def _():
+            matmul(1)
+            finish(n_tiles - 1, 1, False)
+
+        place(2 * n_pairs + 1, 1)
+        place(2 * n_pairs, 0)
 
     @pl.when((n_tiles > 0) & jnp.logical_not(narrow))
     def _():
-        run_tiles(True)
+        def one_tile(i, _):
+            make_hidden(i, 0)
+            matmul(0)
+            finish(i, 0, True)
+            place(i, 0)
+            return 0
+
+        lax.fori_loop(0, n_tiles, one_tile, 0)
+
+    flen = jnp.zeros((OCT, 128), jnp.int32)
+    for b in range(n_utt):
+        flen = jnp.where(lane_utt == b, flen_s[b] - t0, flen)
+    for k in range(n_oct):
+        live = k * OCT + frame8 < flen
+        for u in range(n_pos):
+            rows = slice((k * n_pos + u) * OCT, (k * n_pos + u + 1) * OCT)
+            both = both_d[rows, :]
+            blank_d[rows, :] = jnp.where(live, both, 0.0)
+            label_d[rows, :] = jnp.where(live, pltpu.roll(both, half, 1), NEG_FILL)
 
     entry = frame8 * rep + lane8 % rep
     stay = [jnp.where(entry == u, 0.0, NEG_FILL) for u in range(n_pos)]
@@ -196,22 +228,35 @@
                 alpha = high + jnp.log(1.0 + jnp.exp(low - high))
             stay[u] = alpha + blank_d[row:row + 1, :]
             move[u] = alpha + label_d[row:row + 1, :]
+    n_turn = n_pos // rep
     for u in range(n_pos):
-        for j in range(n_pos // rep):
-            turn_v[GROUP * j + u:GROUP * j + u + 1, :] = stay[u][j:j + 1, :]
-    turned = turn_v[...].T
+        for j in range(n_turn):
+            turn_v[j // 4, GROUP * (j % 4) + u:GROUP * (j % 4) + u + 1, :] = stay[u][j:j + 1, :]
     per = 128 // GROUP
     group = lane8 // GROUP
+    lower = frame8 < rep
+    turned = [turn_v[k].T[:half, :] for k in range(2)]
+    shifted = {}
     for h in range(n_utt // per):
-        for j in range(n_pos // rep):
+        for i in range(n_turn // 2):
             out = None
             for q in range(per):
-                b = per * h + q
-                piece = turned[rep * b:rep * b + rep, :]
-                if q != j:
-                    piece = pltpu.roll(piece, (GROUP * (q - j)) % 128, 1)
+                vreg = (per * h + q) // 2
+                pieces = []
+                for c in range(2):
+                    j = 2 * i + c
+                    key = (j // 4, vreg, (q - j) % 4, (q % 2) != c)
+                    if key not in shifted:
+                        piece = turned[key[0]][8 * vreg:8 * vreg + 8, :]
+                        if key[2]:
+                            piece = pltpu.roll(piece, GROUP * key[2], 1)
+                        if key[3]:
+                            piece = pltpu.roll(piece, rep, 0)
+                        shifted[key] = piece
+                    pieces.append(shifted[key])
+                piece = jnp.where(lower, pieces[0], pieces[1])
                 out = piece if out is None else jnp.where(group == q, piece, out)
-            m_out[h, rep * j:rep * j + rep, :] = out
+            m_out[h, 8 * i:8 * i + 8, :] = out
 
 
 def lattice_kernel(n_seq, m_hbm, llen_hbm, loss_ref,
@@ -332,7 +377,7 @@
     n_oct = t_local // OCT
     n_slab = joint // 128
     per = 128 // GROUP
-    tab_rows = -(-(n_utt * n_pos * n_oct // ITEMS + 1) // 8) * 8
+    tab_rows = -(-(n_utt * n_pos * n_oct // ITEMS + 2) // 8) * 8
     hbm = pl.BlockSpec(memory_space=pl.ANY)
     vmem = pl.BlockSpec(memory_space=pltpu.VMEM)
     f32, bf16, i32 = jnp.float32, jnp.bfloat16, jnp.int32
@@ -353,14 +398,16 @@
             pltpu.SMEM((n_utt,), i32),
             pltpu.SMEM((n_utt,), i32),
             pltpu.VMEM((vocab, joint), bf16),
-            pltpu.VMEM((vocab, 128), f32),
+            pltpu.VMEM((vocab + 8, 128), f32),
             pltpu.VMEM((n_slab, n_utt * t_local, 128), f32),
             pltpu.VMEM((n_slab, n_utt * n_pos, 128), f32),
-            pltpu.VMEM((ITEMS * OCT, joint), bf16),
-            pltpu.VMEM((2, vocab, 128), f32),
+            pltpu.VMEM((2, ITEMS * OCT, joint), bf16),
+            pltpu.VMEM((2, 2, vocab + 8, 128), f32),
+            pltpu.VMEM((2, 2, 8, 128), f32),
             pltpu.VMEM((t_local * n_pos, 128), f32),
             pltpu.VMEM((t_local * n_pos, 128), f32),
-            pltpu.VMEM((128, 128), f32),
+            pltpu.VMEM((t_local * n_pos, 128), f32),
+            pltpu.VMEM((2, 128, 128), f32),
             pltpu.VMEM((2, tab_rows, 128), i32),
             pltpu.SMEM((2, tab_rows, 128), i32),
             pltpu.SemaphoreType.DMA((9,)),

time: 36 us -> 34.9 us (0.969); the launches traced: 36 us -> 35.4 us
  Pallas kernels: 35.4 us -> 34.9 us
    pallas_call x1, Pallas kernels: 19.8 us -> 19.2 us  [joint_call(): pl.pallas_call(joint_kernel, out_shape=pltpu.VMEM((n_utt // per, n_pos, 1...]
where the time goes in v1:
time: 34.9 us; the launch traced here: 35.4 us
  Pallas kernels  34.9 us (100%)
  local copies, waits for them, and re-layouts  0.51 us (1%)
    pallas_call x1, Pallas kernels, joint_call(): pl.pallas_call(joint_kernel, out_shape=pltpu.VMEM((n_utt // per, n_pos, 1...  19.2 us
    pallas_call x1, Pallas kernels, lattice_call(): pl.pallas_call(functools.partial(lattice_kernel, n_seq), out_shape=pltpu....  15.7 us

profile of v1, /device:TPU:21, one launch (start us, length us, event | category | flops | bytes accessed | tf_op | source)
XLA Modules:
  0.0 35.4 jit_solution(14230013667873605319)
XLA Ops:
  0.0 19.2 %joint.1.m_hbm = f32[4,24,128]{2,1,0:T(8,128)S(1)} custom-call(bf16[384,1024]{1,0:T(8,128)(2,1)} %bitcast.3, bf16[384,320]{1,0:T(8,128)(2,1)} %bitcast.4, bf16[1024,512]{1,0:T(8,128)(2,1)} %wenc_hbm.1, bf16[320,512]{1,0:T(8,128)(2,1)} %wpred_hbm.1, bf16[512,1024]{1,0:T(8,128)(2,1)} %wout_hbm.1, f32[8,128]{1,0:T(8,128)} %bitcast.5, s32[16,23]{1,0:T(8,128)} %lab_hbm.1, ...), custom_call_target="tpu_custom_call" | custom-call | tf_op jit(solution)/shard_map/joint/pallas_call | solution.py:384
  19.2 15.7 %lattice.1 = f32[16]{0:T(128)S(1)} custom-call(f32[4,24,128]{2,1,0:T(8,128)S(1)} %joint.1.m_hbm, s32[16]{0:T(128)} %llen_hbm.3), custom_call_target="tpu_custom_call" | custom-call | tf_op jit(solution)/shard_map/lattice/pallas_call | solution.py:425
  34.9 0.5 %copy.11 = f32[16]{0:T(128)} copy(f32[16]{0:T(128)S(1)} %lattice.1) | data formatting | bytes 128
